TPU v7x, 256 devices: a whole 4x4x8 slice. The times are simulated.
256 devices in a mesh: seq: 128 (over z, x, y), dp: 2 (over core).
Axes of the slice: x: 4, y: 4, z: 8, core: 2. Of those that a mesh axis runs over, the one named last changes fastest.
Arguments:
- queries: bfloat16 [2, 24576, 4096], P('dp', 'seq'), may hold values from -6 to 6
- key_vectors: bfloat16 [2, 24576, 4096], P('dp', 'seq'), may hold values from -0.52734375 to 0.52734375
- value_vectors: bfloat16 [2, 24576, 4096], P('dp', 'seq'), may hold values from -6 to 6
- out_grad: bfloat16 [2, 24576, 4096], P('dp', 'seq'), may hold values from -24 to 24
- log_decay: float32 [2, 32, 24576], P('dp', None, 'seq'), may hold values from -0.7729167 to 0, as said below
- norm_gain: float32 [4096], replicated, may hold values from 0.25 to 1.75
Outputs:
- output: bfloat16 [2, 24576, 4096], P('dp', 'seq')
- grad_queries: bfloat16 [2, 24576, 4096], P('dp', 'seq')
- grad_keys: bfloat16 [2, 24576, 4096], P('dp', 'seq')
- grad_values: bfloat16 [2, 24576, 4096], P('dp', 'seq')
- grad_gain: float32 [4096], P('seq')
Inputs may be any that keep to these rules, and one draw needn't show every extreme that they name: `log_decay`: every entry is negative.
All inputs are finite; a program needn't handle non-finite values.
Results may differ from a plain program's by a relative error of at most 0.006.
Values may be sent and summed in bfloat16 or wider, within the bound.
A program may use at most 128 MiB of HBM per device.

v0:
```python
import functools

import jax
import jax.numpy as jnp
from jax import lax
from jax.experimental import pallas as pl
from jax.experimental.pallas import tpu as pltpu
from jax.sharding import Mesh
from jax.sharding import PartitionSpec as P

AXES = ("z", "x", "y", "dp")
SEQ = ("z", "x", "y")
SIZES = {"z": 8, "x": 4, "y": 4, "dp": 2}
NZ, NX, NY = 8, 4, 4
D = 128
OWN = 8
G = 4
HPG = OWN // G
R = HPG * D
RX = R // NX
BF = jnp.bfloat16
F32 = jnp.float32
epsilon = 1e-06


def here():
    return {name: lax.axis_index(name) for name in AXES}


def shifted(me, axis, step):
    there = dict(me)
    there[axis] = lax.rem(me[axis] + step, SIZES[axis])
    return tuple(there[name] for name in AXES)


def push(src, dst, send, recv, target):
    return pltpu.make_async_remote_copy(
        src_ref=src,
        dst_ref=dst,
        send_sem=send,
        recv_sem=recv,
        device_id=target,
        device_id_type=pl.DeviceIdType.MESH,
    )


class Wire:
    def __init__(self, me, axis, sems):
        self.me, self.axis, self.sems = me, axis, sems
        self.steps = range(1, SIZES[axis])
        self.open = []

    def peer(self, step):
        return lax.rem(self.me[self.axis] + step, SIZES[self.axis])

    def send(self, step, key, src, dst):
        send, recv = self.sems
        copy = push(src, dst, send.at[step - 1, key], recv.at[step - 1, key], shifted(self.me, self.axis, step))
        copy.start()
        self.open.append(copy)

    def arrived(self, step, key, dst):
        send, recv = self.sems
        push(dst, dst, send.at[step - 1, key], recv.at[step - 1, key], shifted(self.me, self.axis, step)).wait_recv()

    def drain(self):
        for copy in self.open:
            copy.wait_send()


def sem_pair(axis, keys):
    return [pltpu.SemaphoreType.DMA((SIZES[axis] - 1, keys))] * 2


def slot_of(me, axis, index):
    n = SIZES[axis]
    return lax.rem(me[axis] + (n - 1) + (n - index), n)


def greet(me):
    barrier = pltpu.get_barrier_semaphore()
    count = 0
    for axis in AXES:
        for step in range(1, SIZES[axis]):
            pl.semaphore_signal(
                barrier, inc=1, device_id=shifted(me, axis, step), device_id_type=pl.DeviceIdType.MESH
            )
            count += 1
    return lambda: pl.semaphore_wait(barrier, count)


class Decays:
    scratch = [
        pltpu.VMEM((NY, OWN, D), F32),
        pltpu.VMEM((NX, OWN, D), F32),
        pltpu.VMEM((NZ, OWN, D), F32),
        *sem_pair("y", 1),
        *sem_pair("x", 1),
        *sem_pair("z", 1),
    ]

    def __init__(self, me, refs, total):
        self.me, self.total = me, total
        self.levels = dict(zip("yxz", refs[:3]))
        self.wires = {a: Wire(me, a, refs[3 + 2 * i : 5 + 2 * i]) for i, a in enumerate("yxz")}

    def start(self):
        level, wire = self.levels["y"], self.wires["y"]
        for step in wire.steps:
            wire.send(step, 0, self.total.at[wire.peer(step)], level.at[step - 1])
        level[NY - 1] = self.total[self.me["y"]]

    def settle(self, axis):
        for step in self.wires[axis].steps:
            self.wires[axis].arrived(step, 0, self.levels[axis].at[step - 1])

    def lift(self, low, high):
        self.settle(low)
        n, m = SIZES[low], SIZES[high]
        level, above, wire = self.levels[low], self.levels[high], self.wires[high]
        above[m - 1] = functools.reduce(jnp.add, [level[slot_of(self.me, low, k)] for k in range(n)])
        for step in wire.steps:
            wire.send(step, 0, above.at[m - 1], above.at[step - 1])

    def row(self, axis, slot, head):
        return jnp.exp(self.levels[axis][slot, pl.ds(head, 1), :])

    def drain(self):
        for wire in self.wires.values():
            wire.drain()


class Scan:
    scratch = [
        pltpu.VMEM((NY, G, R, D), BF),
        pltpu.VMEM((NX, G, RX, D), BF),
        pltpu.VMEM((NX, G, RX, D), BF),
        pltpu.VMEM((NZ, G, RX, D), BF),
        pltpu.VMEM((NX, G, RX, D), BF),
        pltpu.VMEM((G, NX, RX, D), BF),
        pltpu.VMEM((NY, G, R, D), BF),
        *sem_pair("y", G),
        *sem_pair("x", G),
        *sem_pair("z", G),
        *sem_pair("x", G),
        *sem_pair("y", G),
    ]

    def __init__(self, me, refs, decays, prior, backward):
        self.me, self.decays, self.prior, self.backward = me, decays, prior, backward
        self.yin, self.xin, self.xout, self.zin, self.lines, self.line, self.yout = refs[:7]
        sems = refs[7:]
        names = ("y", "x", "z", "x", "y")
        self.y, self.x, self.z, self.xback, self.yback = [
            Wire(me, a, sems[2 * i : 2 * i + 2]) for i, a in enumerate(names)
        ]

    def order(self, n):
        return list(range(n))[:: -1 if self.backward else 1]

    def start(self, g, source):
        for step in self.y.steps:
            self.y.send(step, g, source(self.y.peer(step)), self.yin.at[step - 1, g])

    def over_lines(self, g):
        me = self.me
        for step in self.y.steps:
            self.y.arrived(step, g, self.yin.at[step - 1, g])
        for i in range(HPG):
            rows = pl.ds(i * D, D)
            total = None
            for k in self.order(NY):
                slot = slot_of(me, "y", k)
                term = self.yin[slot, g, rows, :].astype(F32)
                total = term if total is None else total * self.decays.row("y", slot, g * HPG + i) + term
            total = total.astype(BF)
            if RX >= D:
                per = RX // D
                self.xout[i // per, g, pl.ds((i % per) * D, D), :] = total
            else:
                per = D // RX
                for j in range(per):
                    self.xout[i * per + j, g] = total[j * RX : (j + 1) * RX]
        for step in self.x.steps:
            self.x.send(step, g, self.xout.at[self.x.peer(step), g], self.xin.at[step - 1, g])
        self.xin[NX - 1, g] = self.xout[me["x"], g]

    def pieces(self, g):
        first = g * HPG + (self.me["x"] * RX) // D
        return [(first + i, pl.ds(i * D, min(D, RX))) for i in range(max(1, RX // D))]

    def over_planes(self, g):
        me = self.me
        for step in self.x.steps:
            self.x.arrived(step, g, self.xin.at[step - 1, g])
        for head, rows in self.pieces(g):
            total = None
            for k in self.order(NX):
                slot = slot_of(me, "x", k)
                term = self.xin[slot, g, rows, :].astype(F32)
                total = term if total is None else total * self.decays.row("x", slot, head) + term
            self.zin[NZ - 1, g, rows, :] = total.astype(BF)
        for step in self.z.steps:
            self.z.send(step, g, self.zin.at[NZ - 1, g], self.zin.at[step - 1, g])

    def before_lines(self, g):
        me = self.me
        for step in self.z.steps:
            self.z.arrived(step, g, self.zin.at[step - 1, g])
        for head, rows in self.pieces(g):
            state = jnp.zeros((min(D, RX), D), F32)
            for k in self.order(NZ):
                slot = slot_of(me, "z", k)
                passed = (k > me["z"]) if self.backward else (k < me["z"])
                ahead = state * self.decays.row("z", slot, head) + self.zin[slot, g, rows, :].astype(F32)
                state = jnp.where(passed, ahead, state)
            for n, k in enumerate(self.order(NX)):
                self.lines[k, g, rows, :] = state.astype(BF)
                if n < NX - 1:
                    slot = slot_of(me, "x", k)
                    state = state * self.decays.row("x", slot, head) + self.xin[slot, g, rows, :].astype(F32)
        for step in self.xback.steps:
            self.xback.send(step, g, self.lines.at[self.xback.peer(step), g], self.line.at[g, me["x"]])
        self.line[g, me["x"]] = self.lines[me["x"], g]

    def before_blocks(self, g):
        me = self.me
        for step in self.xback.steps:
            self.xback.arrived(step, g, self.line.at[g, lax.rem(me["x"] + (NX - step), NX)])
        for i in range(HPG):
            rows = pl.ds(i * D, D)
            if RX >= D:
                per = RX // D
                state = self.line[g, i // per, pl.ds((i % per) * D, D), :].astype(F32)
            else:
                per = D // RX
                state = jnp.concatenate([self.line[g, i * per + j].astype(F32) for j in range(per)], axis=0)
            for n, k in enumerate(self.order(NY)):
                self.yout[k, g, rows, :] = state.astype(BF)
                if n < NY - 1:
                    slot = slot_of(me, "y", k)
                    row = self.decays.row("y", slot, g * HPG + i)
                    state = state * row + self.yin[slot, g, rows, :].astype(F32)
        for step in self.yback.steps:
            self.yback.send(step, g, self.yout.at[self.yback.peer(step), g], self.prior.at[me["y"], g])
        self.prior[me["y"], g] = self.yout[me["y"], g]

    def arrive(self, g, step):
        self.yback.arrived(step, g, self.prior.at[lax.rem(self.me["y"] + (NY - step), NY), g])

    def drain(self):
        for wire in (self.y, self.x, self.z, self.xback, self.yback):
            wire.drain()


class Gain:
    scratch = [
        pltpu.VMEM((NZ, 4, 8, D), F32),
        pltpu.VMEM((4, 8, D), F32),
        pltpu.VMEM((NX, 8, D), F32),
        pltpu.VMEM((NY, 8, D), F32),
        pltpu.VMEM((2, 8, D), F32),
        *sem_pair("z", 1),
        *sem_pair("x", 1),
        *sem_pair("y", 1),
        *sem_pair("dp", 1),
    ]

    def __init__(self, me, refs, part, out):
        self.me, self.part, self.out = me, part, out
        self.zin, self.plane, self.xin, self.yin, self.din = refs[:5]
        sems = refs[5:]
        self.z, self.x, self.y, self.dp = [
            Wire(me, a, sems[2 * i : 2 * i + 2]) for i, a in enumerate(("z", "x", "y", "dp"))
        ]

    def start(self):
        for step in self.z.steps:
            self.z.send(step, 0, self.part.at[pl.ds(4 * self.z.peer(step), 4)], self.zin.at[step - 1])
        self.zin[NZ - 1] = self.part[pl.ds(4 * self.me["z"], 4)]

    def total(self, wire, buffer):
        n = SIZES[wire.axis]
        for step in wire.steps:
            wire.arrived(step, 0, buffer.at[step - 1])
        return functools.reduce(jnp.add, [buffer[slot_of(self.me, wire.axis, k)] for k in range(n)])

    def over_z(self):
        self.plane[...] = self.total(self.z, self.zin)
        for step in self.x.steps:
            self.x.send(step, 0, self.plane.at[self.x.peer(step)], self.xin.at[step - 1])
        self.xin[NX - 1] = self.plane[self.me["x"]]

    def over_x(self):
        self.yin[NY - 1] = self.total(self.x, self.xin)
        for step in self.y.steps:
            self.y.send(step, 0, self.yin.at[NY - 1], self.yin.at[step - 1])

    def over_y(self):
        self.din[1] = self.total(self.y, self.yin)
        self.dp.send(1, 0, self.din.at[1], self.din.at[0])

    def over_dp(self):
        row = jnp.sum(self.total(self.dp, self.din), axis=0, keepdims=True)
        width = D // NY
        self.out[...] = functools.reduce(
            jnp.add,
            [
                jnp.where(self.me["y"] == k, row[:, k * width : (k + 1) * width], 0.0)
                for k in range(NY)
            ],
        )

    def drain(self):
        for wire in (self.z, self.x, self.y, self.dp):
            wire.drain()


T = 192
HEADS = NY * OWN

CHAIN = (
    ("local", 1.0, "y", 2.9),
    ("lines", 0.35, "x", 2.7),
    ("planes", 0.15, "z", 4.0),
    ("before_lines", 0.25, "x", 2.7),
    ("before_blocks", 0.5, "y", 2.9),
    ("middle", 2.2, "y", 2.9),
    ("back_lines", 0.35, "x", 2.7),
    ("back_planes", 0.15, "z", 4.0),
    ("back_before_lines", 0.25, "x", 2.7),
    ("back_before_blocks", 0.5, "y", 2.9),
    ("last", 1.5, None, 0.0),
)
BUSY = {"y": 11.5 / G, "x": 2.9 / G, "z": 11.5 / G}
FILL = (("early", "middle", 1.8), ("late", "last", 1.8))


def plan():
    rest = [sum(c[1] + c[3] for c in CHAIN[i:]) for i in range(len(CHAIN))]
    step_of = {c[0]: i for i, c in enumerate(CHAIN)}
    now, at, ready = 0.0, [0] * G, [0.0] * G
    links = {"y": 0.0, "x": 0.0, "z": 0.0}
    filled, order = set(), []
    after = {"early": -1, "late": step_of["middle"]}
    while any(a < len(CHAIN) for a in at):
        fits = []
        for g in range(G):
            if at[g] == len(CHAIN):
                continue
            name = CHAIN[at[g]][0]
            if ready[g] <= now:
                lacking = [f for f, s, _ in FILL if s == name and (f, g) not in filled]
                fits.append((-rest[at[g]], g, lacking[0] if lacking else name))
        if fits:
            _, g, name = min(fits)
        else:
            spare = [
                (g, f) for f, s, _ in FILL for g in range(G) if (f, g) not in filled and at[g] > after[f]
            ]
            if not spare:
                now = min(ready[g] for g in range(G) if at[g] < len(CHAIN))
                continue
            g, name = min(spare, key=lambda s: (s[1] != "early", s[0]))
        order.append((name, g))
        if name in after:
            filled.add((name, g))
            now += [c for f, _, c in FILL if f == name][0]
            continue
        _, cost, link, way = CHAIN[at[g]]
        now += cost
        at[g] += 1
        ready[g] = now
        if link:
            links[link] = max(now, links[link]) + BUSY[link]
            ready[g] = links[link] + way
    return order, now


def cols(head):
    return pl.ds(pl.multiple_of(head * D, D), D)


def mm(a, b, da, db):
    return lax.dot_general(a, b, (((da,), (db,)), ((), ())), preferred_element_type=F32)


def kernel(q, k, v, g_out, log_decay, gain, out, gq, gk, gv, gain_sum, *refs):
    nd, ns, ng = len(Decays.scratch), len(Scan.scratch), len(Gain.scratch)
    total, cum, cums, inside, wts, ga, gkp, gvp, part, local, prior, later_local, later = refs[:13]
    refs = refs[13:]
    me = here()
    decays = Decays(me, refs[:nd], total)
    refs = refs[nd:]
    fore = Scan(me, refs[:ns], decays, prior, False)
    back = Scan(me, refs[ns : 2 * ns], decays, later, True)
    sums = Gain(me, refs[2 * ns :], part, gain_sum)

    met = greet(me)
    upper = (
        lax.broadcasted_iota(jnp.int32, (T, T), 0) <= lax.broadcasted_iota(jnp.int32, (T, T), 1)
    ).astype(F32)
    running = lax.dot_general(
        log_decay[...], upper, (((1,), (0,)), ((), ())), precision=lax.Precision.HIGHEST, preferred_element_type=F32
    )
    cum[...] = running
    blocks = jnp.broadcast_to(running[:, T - 1 : T], (HEADS, D))
    for j in range(NY):
        total[j] = blocks[j * OWN : (j + 1) * OWN]

    def for_heads(g, work):
        def step(d, carry):
            j = lax.rem(me["y"] + 1 + d, NY)
            for i in range(HPG):
                work(j, i, j * OWN + g * HPG + i)
            return carry

        lax.fori_loop(0, NY, step, 0)

    def weight(head):
        by_row = cums[head]
        gap = jnp.concatenate([by_row, by_row[:, : T - D]], axis=1) - cum[pl.ds(head, 1), :]
        causal = lax.broadcasted_iota(jnp.int32, (T, T), 0) >= lax.broadcasted_iota(jnp.int32, (T, T), 1)
        return jnp.exp(jnp.where(causal, gap, -1e30))

    def end_scale(head):
        by_row = cums[head]
        return jnp.exp(by_row[T - 1 : T, :] - by_row)

    def local_of(g):
        def work(j, i, head):
            by_row = jnp.transpose(jnp.broadcast_to(cum[pl.ds(head, 1), :], (D, T)))
            cums[head] = by_row
            scale = jnp.exp(by_row[T - 1 : T, :] - by_row)
            decayed = (k[:, cols(head)].astype(F32) * scale).astype(BF)
            local[j, g, pl.ds(i * D, D), :] = mm(decayed, v[:, cols(head)], 0, 0).astype(BF)

        for_heads(g, work)
        fore.yin[NY - 1, g] = local[me["y"], g]

    def early(g):
        def work(j, i, head):
            scores = mm(q[:, cols(head)], k[:, cols(head)], 1, 1)
            weighted = (scores * weight(head)).astype(BF)
            wts[head] = weighted
            inside[head] = mm(weighted, v[:, cols(head)], 1, 0)

        for_heads(g, work)

    def middle(g):
        for step in fore.yback.steps:
            fore.arrive(g, step)

        def work(j, i, head):
            state = prior[j, g, pl.ds(i * D, D), :]
            start = jnp.exp(cums[head])
            qh = q[:, cols(head)]
            attended = inside[head] + mm(qh, state, 1, 0) * start
            inv = lax.rsqrt(jnp.mean(attended * attended, axis=1, keepdims=True) + epsilon)
            normed = attended * inv
            row = gain[pl.ds(head, 1), :]
            out[:, cols(head)] = (normed * row).astype(BF)
            grad = g_out[:, cols(head)].astype(F32)
            scaled = grad * row
            lean = jnp.mean(scaled * normed, axis=1, keepdims=True)
            attended_grad = (inv * (scaled - normed * lean)).astype(BF)
            ga[head] = attended_grad
            part[head] = jnp.sum((grad * normed).reshape(T // 8, 8, D), axis=0)
            decayed = (qh.astype(F32) * start).astype(BF)
            later_local[j, g, pl.ds(i * D, D), :] = mm(decayed, attended_grad, 0, 0).astype(BF)

        for_heads(g, work)
        back.start(g, lambda peer: later_local.at[peer, g])
        back.yin[NY - 1, g] = later_local[me["y"], g]

    def late(g):
        def work(j, i, head):
            grad = ga[head]
            grad_scores = mm(grad, v[:, cols(head)], 1, 1)
            gw = (grad_scores * weight(head)).astype(BF)
            state = prior[j, g, pl.ds(i * D, D), :]
            gq[:, cols(head)] = (mm(gw, k[:, cols(head)], 1, 0) + jnp.exp(cums[head]) * mm(grad, state, 1, 1)).astype(BF)
            gkp[head] = mm(gw, q[:, cols(head)], 0, 0)
            gvp[head] = mm(wts[head], grad, 0, 0)

        for_heads(g, work)

    def last(g):
        for step in back.yback.steps:
            back.arrive(g, step)

        def work(j, i, head):
            state = later[j, g, pl.ds(i * D, D), :]
            scale = end_scale(head)
            gk[:, cols(head)] = (gkp[head] + scale * mm(v[:, cols(head)], state, 1, 1)).astype(BF)
            gv[:, cols(head)] = (gvp[head] + scale * mm(k[:, cols(head)], state, 1, 0)).astype(BF)

        for_heads(g, work)

    stages = {
        "early": early,
        "lines": fore.over_lines,
        "planes": fore.over_planes,
        "before_lines": fore.before_lines,
        "before_blocks": fore.before_blocks,
        "middle": middle,
        "late": late,
        "back_lines": back.over_lines,
        "back_planes": back.over_planes,
        "back_before_lines": back.before_lines,
        "back_before_blocks": back.before_blocks,
        "last": last,
    }
    order, _ = plan()
    levels = [lambda: decays.lift("y", "x"), lambda: decays.lift("x", "z"), lambda: decays.settle("z")]
    needs = {"lines": 1, "planes": 2, "before_lines": 3}
    folds = [sums.over_z, sums.over_x, sums.over_y, sums.over_dp]
    to_open = True
    middles = 0
    for name, g in order:
        if name == "local":
            local_of(g)
            if to_open:
                met()
                decays.start()
                to_open = False
            fore.start(g, lambda peer: local.at[peer, g])
            continue
        while levels and needs.get(name, 0) > 3 - len(levels):
            levels.pop(0)()
        stages[name](g)
        if name == "middle":
            middles += 1
            if middles == G:
                sums.start()
        elif middles == G and folds and name == "back_before_lines":
            folds.pop(0)()
        elif middles == G and folds and name == "last":
            folds.pop(0)()
    for fold in folds:
        fold()
    decays.drain()
    fore.drain()
    back.drain()
    sums.drain()


def body(queries, key_vectors, value_vectors, out_grad, log_decay, norm_gain):
    shape = queries.shape
    wide = shape[-1]
    vmem = pl.BlockSpec(memory_space=pltpu.VMEM)
    scratch = [
        pltpu.VMEM((NY, OWN, D), F32),
        pltpu.VMEM((HEADS, T), F32),
        pltpu.VMEM((HEADS, T, D), F32),
        pltpu.VMEM((HEADS, T, D), F32),
        pltpu.VMEM((HEADS, T, T), BF),
        pltpu.VMEM((HEADS, T, D), BF),
        pltpu.VMEM((HEADS, T, D), F32),
        pltpu.VMEM((HEADS, T, D), F32),
        pltpu.VMEM((HEADS, 8, D), F32),
        pltpu.VMEM((NY, G, R, D), BF),
        pltpu.VMEM((NY, G, R, D), BF),
        pltpu.VMEM((NY, G, R, D), BF),
        pltpu.VMEM((NY, G, R, D), BF),
    ]
    rows = jax.ShapeDtypeStruct((T, wide), BF)
    results = pl.pallas_call(
        kernel,
        out_shape=[rows] * 4 + [jax.ShapeDtypeStruct((1, D // NY), F32)],
        in_specs=[vmem] * 6,
        out_specs=[vmem] * 5,
        scratch_shapes=scratch + Decays.scratch + Scan.scratch * 2 + Gain.scratch,
        compiler_params=pltpu.CompilerParams(
            collective_id=0, has_side_effects=True, vmem_limit_bytes=60 * 1024 * 1024
        ),
        name="attention",
    )(
        *[a.reshape(T, wide) for a in (queries, key_vectors, value_vectors, out_grad)],
        log_decay.reshape(HEADS, T),
        norm_gain.reshape(HEADS, D),
    )
    return (*[r.reshape(shape) for r in results[:4]], results[4].reshape(D // NY))


def solution(mesh):
    split = Mesh(mesh.devices.reshape(NZ, NX, NY, mesh.shape["dp"]), AXES)
    rows = P("dp", SEQ, None)
    return jax.shard_map(
        body,
        mesh=split,
        in_specs=(rows, rows, rows, rows, P("dp", None, SEQ), P()),
        out_specs=(rows, rows, rows, rows, P(SEQ)),
        check_vma=False,
    )
```

profile of v0, /device:TPU:2, one launch (start us, length us, event | category | flops | bytes accessed | tf_op | source)
XLA Modules:
  0.0 103.1 jit_solution(5191054217898744771)
XLA Ops:
  0.6 94.0 %attention.1 = (bf16[192,4096]{1,0:T(8,128)(2,1)}, bf16[192,4096]{1,0:T(8,128)(2,1)}, bf16[192,4096]{1,0:T(8,128)(2,1)}, bf16[192,4096]{1,0:T(8,128)(2,1)}, f32[1,32]{1,0:T(1,128)}) custom-call(bf16[192,4096]{1,0:T(8,128)(2,1)} %bitcast.15, bf16[192,4096]{1,0:T(8,128)(2,1)} %bitcast.16, bf16[192,4096]{1,0:T(8,128)(2,1)} %bitcast.17, ...), custom_call_target="tpu_custom_call" | custom-call | tf_op jit(solution)/shard_map/attention/pallas_call | solution.py:568
  94.6 0.0 copy-start.2
  94.6 2.8 %copy.16 = bf16[1,192,4096]{2,1,0:T(8,128)(2,1)} copy(bf16[1,192,4096]{2,1,0:T(8,128)(2,1)} %bitcast.14) | data formatting | bytes 3145728
  97.4 0.0 copy-done.2
  97.4 0.0 copy-start.1
  97.4 1.1 %copy.17 = bf16[1,192,4096]{2,1,0:T(8,128)(2,1)} copy(bf16[1,192,4096]{2,1,0:T(8,128)(2,1)S(1)} %bitcast.13) | data formatting | bytes 3145728
  98.6 0.8 copy-done.1
  99.4 0.0 copy-start
  99.4 1.1 %copy.18 = bf16[1,192,4096]{2,1,0:T(8,128)(2,1)} copy(bf16[1,192,4096]{2,1,0:T(8,128)(2,1)S(1)} %bitcast.12) | data formatting | bytes 3145728
  100.6 0.8 copy-done
  101.4 0.0 copy-start.3
  101.4 1.1 %copy.19 = bf16[1,192,4096]{2,1,0:T(8,128)(2,1)} copy(bf16[1,192,4096]{2,1,0:T(8,128)(2,1)S(1)} %bitcast.11) | data formatting | bytes 3145728
  102.5 0.0 copy-done.3
  102.5 0.5 copy.20
Async XLA Ops:
  94.6 2.8 %copy-start.2 = (bf16[192,4096]{1,0:T(8,128)(2,1)S(1)}, bf16[192,4096]{1,0:T(8,128)(2,1)}, u32[]{:S(2)}) copy-start(bf16[192,4096]{1,0:T(8,128)(2,1)} %get-tuple-element.11) | copy-start | bytes 4718596
  97.4 2.0 %copy-start.1 = (bf16[192,4096]{1,0:T(8,128)(2,1)S(1)}, bf16[192,4096]{1,0:T(8,128)(2,1)}, u32[]{:S(2)}) copy-start(bf16[192,4096]{1,0:T(8,128)(2,1)} %get-tuple-element.12) | copy-start | bytes 4718596
  99.4 2.0 %copy-start = (bf16[192,4096]{1,0:T(8,128)(2,1)S(1)}, bf16[192,4096]{1,0:T(8,128)(2,1)}, u32[]{:S(2)}) copy-start(bf16[192,4096]{1,0:T(8,128)(2,1)} %get-tuple-element.13) | copy-start | bytes 4718596
  101.4 1.1 %copy-start.3 = (f32[1,32]{1,0:T(1,128)S(1)}, f32[1,32]{1,0:T(1,128)}, u32[]{:S(2)}) copy-start(f32[1,32]{1,0:T(1,128)} %get-tuple-element.14) | copy-start | bytes 388
where the time goes:
time: 104 us; the launch traced here: 103 us
  Pallas kernels  94 us (90%)
  local copies, waits for them, and re-layouts  8.43 us (8%)
    pallas_call x1, Pallas kernels, body(): pl.pallas_call(kernel, out_shape=[rows] * 4 + [jax.ShapeDtypeStruct((1, D...  94 us
    unnamed x13, local copies, waits for them, and re-layouts  8.43 us

commit v1 on v0

v1 whole, which is shorter than its diff:
```python
import functools

import jax
import jax.numpy as jnp
from jax import lax
from jax.experimental import pallas as pl
from jax.experimental.pallas import tpu as pltpu
from jax.sharding import Mesh
from jax.sharding import PartitionSpec as P

AXES = ("z", "x", "y", "dp")
SEQ = ("z", "x", "y")
SIZES = {"z": 8, "x": 4, "y": 4, "dp": 2}
NZ, NX, NY = 8, 4, 4
D = 128
OWN = 8
G = 8
HPG = OWN // G
AT_ONCE = min(NY, 4 // HPG)
R = HPG * D
RX = R // NX
BF = jnp.bfloat16
F32 = jnp.float32
epsilon = 1e-06


def here():
    return {name: lax.axis_index(name) for name in AXES}


def shifted(me, axis, step):
    there = dict(me)
    there[axis] = lax.rem(me[axis] + step, SIZES[axis])
    return tuple(there[name] for name in AXES)


def push(src, dst, send, recv, target):
    return pltpu.make_async_remote_copy(
        src_ref=src,
        dst_ref=dst,
        send_sem=send,
        recv_sem=recv,
        device_id=target,
        device_id_type=pl.DeviceIdType.MESH,
    )


class Wire:
    def __init__(self, me, axis, sems):
        self.me, self.axis, self.sems = me, axis, sems
        self.peers = SIZES[axis] - 1
        self.sent = []

    def peer(self, step):
        return lax.rem(self.me[self.axis] + step, SIZES[self.axis])

    def send(self, key, source, slots):
        for step in range(1, self.peers + 1):
            push(
                source(self.peer(step)),
                slots.at[step - 1],
                self.sems[0].at[key],
                self.sems[1].at[key],
                shifted(self.me, self.axis, step),
            ).start()
        self.sent.append((key, slots))

    def _all(self, key, slots):
        taken = slots.at[pl.ds(0, self.peers)]
        return push(taken, taken, self.sems[0].at[key], self.sems[1].at[key], shifted(self.me, self.axis, 1))

    def arrived(self, key, slots):
        self._all(key, slots).wait_recv()

    def drain(self):
        for key, slots in self.sent:
            self._all(key, slots).wait_send()
        self.sent = []


def sem_pair(keys):
    return [pltpu.SemaphoreType.DMA((keys,))] * 2


def slot_of(me, axis, index):
    n = SIZES[axis]
    return lax.rem(me[axis] + (n - 1) + (n - index), n)


def greet(me):
    barrier = pltpu.get_barrier_semaphore()
    count = 0
    for axis in AXES:
        for step in range(1, SIZES[axis]):
            pl.semaphore_signal(
                barrier, inc=1, device_id=shifted(me, axis, step), device_id_type=pl.DeviceIdType.MESH
            )
            count += 1
    return lambda: pl.semaphore_wait(barrier, count)


class Decays:
    scratch = [
        pltpu.VMEM((NY, OWN, D), F32),
        pltpu.VMEM((NX, OWN, D), F32),
        pltpu.VMEM((NZ, OWN, D), F32),
        *sem_pair(1) * 3,
    ]

    def __init__(self, me, refs, total):
        self.me, self.total = me, total
        self.levels = dict(zip("yxz", refs[:3]))
        self.wires = {a: Wire(me, a, refs[3 + 2 * i : 5 + 2 * i]) for i, a in enumerate("yxz")}

    def start(self):
        level = self.levels["y"]
        self.wires["y"].send(0, lambda peer: self.total.at[peer], level)
        level[NY - 1] = self.total[self.me["y"]]

    def settle(self, axis):
        self.wires[axis].arrived(0, self.levels[axis])

    def lift(self, low, high):
        self.settle(low)
        n, m = SIZES[low], SIZES[high]
        level, above = self.levels[low], self.levels[high]
        above[m - 1] = functools.reduce(jnp.add, [level[slot_of(self.me, low, k)] for k in range(n)])
        self.wires[high].send(0, lambda peer: above.at[m - 1], above)

    def row(self, axis, slot, head):
        return jnp.exp(self.levels[axis][slot, pl.ds(head, 1), :])

    def drain(self):
        for wire in self.wires.values():
            wire.drain()


class Scan:
    scratch = [
        pltpu.VMEM((G, NY, R, D), BF),
        pltpu.VMEM((G, NX, RX, D), BF),
        pltpu.VMEM((G, NX, RX, D), BF),
        pltpu.VMEM((G, NZ, RX, D), BF),
        pltpu.VMEM((G, NX, RX, D), BF),
        pltpu.VMEM((G, NX, RX, D), BF),
        pltpu.VMEM((G, NY, R, D), BF),
        *sem_pair(G) * 5,
    ]

    def __init__(self, me, refs, decays, prior, backward):
        self.me, self.decays, self.prior, self.backward = me, decays, prior, backward
        self.yin, self.xin, self.xout, self.zin, self.lines, self.line, self.yout = refs[:7]
        sems = refs[7:]
        names = ("y", "x", "z", "x", "y")
        self.y, self.x, self.z, self.xback, self.yback = [
            Wire(me, a, sems[2 * i : 2 * i + 2]) for i, a in enumerate(names)
        ]

    def order(self, n):
        return list(range(n))[:: -1 if self.backward else 1]

    def start(self, g, states):
        self.y.send(g, lambda peer: states.at[peer, g], self.yin.at[g])
        self.yin[g, NY - 1] = states[self.me["y"], g]

    def over_lines(self, g):
        me = self.me
        self.y.arrived(g, self.yin.at[g])
        for i in range(HPG):
            rows = pl.ds(i * D, D)
            total = None
            for k in self.order(NY):
                slot = slot_of(me, "y", k)
                term = self.yin[g, slot, rows, :].astype(F32)
                total = term if total is None else total * self.decays.row("y", slot, g * HPG + i) + term
            total = total.astype(BF)
            if RX >= D:
                per = RX // D
                self.xout[g, i // per, pl.ds((i % per) * D, D), :] = total
            else:
                per = D // RX
                for j in range(per):
                    self.xout[g, i * per + j] = total[j * RX : (j + 1) * RX]
        self.x.send(g, lambda peer: self.xout.at[g, peer], self.xin.at[g])
        self.xin[g, NX - 1] = self.xout[g, me["x"]]

    def pieces(self, g):
        first = g * HPG + (self.me["x"] * RX) // D
        return [(first + i, pl.ds(i * D, min(D, RX))) for i in range(max(1, RX // D))]

    def over_planes(self, g):
        me = self.me
        self.x.arrived(g, self.xin.at[g])
        for head, rows in self.pieces(g):
            total = None
            for k in self.order(NX):
                slot = slot_of(me, "x", k)
                term = self.xin[g, slot, rows, :].astype(F32)
                total = term if total is None else total * self.decays.row("x", slot, head) + term
            self.zin[g, NZ - 1, rows, :] = total.astype(BF)
        self.z.send(g, lambda peer: self.zin.at[g, NZ - 1], self.zin.at[g])

    def before_lines(self, g):
        me = self.me
        self.z.arrived(g, self.zin.at[g])
        for head, rows in self.pieces(g):
            state = jnp.zeros((min(D, RX), D), F32)
            for k in self.order(NZ):
                slot = slot_of(me, "z", k)
                passed = (k > me["z"]) if self.backward else (k < me["z"])
                ahead = state * self.decays.row("z", slot, head) + self.zin[g, slot, rows, :].astype(F32)
                state = jnp.where(passed, ahead, state)
            for n, k in enumerate(self.order(NX)):
                self.lines[g, k, rows, :] = state.astype(BF)
                if n < NX - 1:
                    slot = slot_of(me, "x", k)
                    state = state * self.decays.row("x", slot, head) + self.xin[g, slot, rows, :].astype(F32)
        self.xback.send(g, lambda peer: self.lines.at[g, peer], self.line.at[g])
        self.line[g, NX - 1] = self.lines[g, me["x"]]

    def before_blocks(self, g):
        me = self.me
        self.xback.arrived(g, self.line.at[g])
        for i in range(HPG):
            rows = pl.ds(i * D, D)
            if RX >= D:
                per = RX // D
                slot = slot_of(me, "x", i // per)
                state = self.line[g, slot, pl.ds((i % per) * D, D), :].astype(F32)
            else:
                per = D // RX
                state = jnp.concatenate(
                    [self.line[g, slot_of(me, "x", i * per + j)].astype(F32) for j in range(per)], axis=0
                )
            for n, k in enumerate(self.order(NY)):
                self.yout[g, k, rows, :] = state.astype(BF)
                if n < NY - 1:
                    slot = slot_of(me, "y", k)
                    row = self.decays.row("y", slot, g * HPG + i)
                    state = state * row + self.yin[g, slot, rows, :].astype(F32)
        self.yback.send(g, lambda peer: self.yout.at[g, peer], self.prior.at[g])
        self.prior[g, NY - 1] = self.yout[g, me["y"]]

    def arrive(self, g):
        self.yback.arrived(g, self.prior.at[g])

    def drain(self):
        for wire in (self.y, self.x, self.z, self.xback, self.yback):
            wire.drain()


class Gain:
    AXES = ("z", "x", "y", "dp")
    scratch = [*[pltpu.VMEM((SIZES[a], 8, D), F32) for a in AXES], *sem_pair(1) * 4]

    def __init__(self, me, refs, part, out):
        self.me, self.part, self.out = me, part, out
        self.levels = dict(zip(self.AXES, refs[:4]))
        self.wires = {a: Wire(me, a, refs[4 + 2 * i : 6 + 2 * i]) for i, a in enumerate(self.AXES)}

    def start(self):
        self.wires["z"].send(0, lambda peer: self.part.at[peer], self.levels["z"])
        self.levels["z"][NZ - 1] = self.part[self.me["z"]]

    def fold(self, axis):
        n, level = SIZES[axis], self.levels[axis]
        self.wires[axis].arrived(0, level)
        total = functools.reduce(jnp.add, [level[slot_of(self.me, axis, k)] for k in range(n)])
        if axis != "dp":
            above = self.AXES[self.AXES.index(axis) + 1]
            held, m = self.levels[above], SIZES[above]
            held[m - 1] = total
            self.wires[above].send(0, lambda peer: held.at[m - 1], held)
            return
        width = D // NY
        mine = lax.broadcasted_iota(jnp.int32, (8, D), 0) == self.me["x"]
        row = jnp.sum(jnp.where(mine, total, 0.0), axis=0, keepdims=True)
        self.out[...] = functools.reduce(
            jnp.add,
            [jnp.where(self.me["y"] == k, row[:, k * width : (k + 1) * width], 0.0) for k in range(NY)],
        )

    def drain(self):
        for wire in self.wires.values():
            wire.drain()


T = 192
HEADS = NY * OWN

PER = 4 / G
CHAIN = (
    ("local", 0.87 * PER, "y", 4.9),
    ("lines", 0.06, "x", 4.5),
    ("planes", 0.06, "z", 4.3),
    ("before_lines", 0.07, "x", 3.3),
    ("before_blocks", 0.07, "y", 2.4),
    ("middle", 2.1 * PER, "y", 4.2),
    ("back_lines", 0.06, "x", 4.5),
    ("back_planes", 0.06, "z", 4.3),
    ("back_before_lines", 0.07, "x", 3.5),
    ("back_before_blocks", 0.07, "y", 2.8),
    ("last", 0.6 * PER, None, 0.0),
)
BUSY = {"y": 11.3 / G, "x": 2.9 / G, "z": 11.3 / G}
EARLY, LATE = (1, 2) if G > 4 else (2, 2)
FILL = {f"early{n}": ("middle", 1.1 * PER / EARLY) for n in range(EARLY)} | {
    f"late{n}": ("last", 2.7 * PER / LATE) for n in range(LATE)
}
GAIN = (("gain", 4.8), ("gain_z", 4.0), ("gain_x", 4.0), ("gain_y", 2.0), ("gain_dp", 0.0))
MARGIN = 2.0


def plan():
    rest = [sum(c[1] + c[3] for c in CHAIN[i:]) for i in range(len(CHAIN))]
    step_of = {c[0]: i for i, c in enumerate(CHAIN)}
    now, at, ready = 0.0, [0] * G, [0.0] * G
    links = {"y": 0.0, "x": 0.0, "z": 0.0}
    filled, order = set(), []
    summed, sums_ready = 0, None
    while any(a < len(CHAIN) for a in at):
        fits = []
        for g in range(G):
            if at[g] < len(CHAIN) and ready[g] <= now:
                name = CHAIN[at[g]][0]
                lacking = [f for f in FILL if FILL[f][0] == name and (f, g) not in filled]
                fits.append((-rest[at[g]], g, lacking[0] if lacking else name))
        if fits:
            _, g, name = min(fits)
        elif sums_ready is not None and summed < len(GAIN) and sums_ready <= now:
            order.append((GAIN[summed][0], 0))
            sums_ready = now + GAIN[summed][1] + MARGIN
            summed += 1
            now += 0.1
            continue
        else:
            soon = min(ready[g] for g in range(G) if at[g] < len(CHAIN))
            spare = [
                (not f.startswith("early"), g, f)
                for f in FILL
                for g in range(G)
                if (f, g) not in filled and at[g] > (0 if f.startswith("early") else step_of["middle"])
                if now + FILL[f][1] <= soon + 0.15
            ]
            if not spare:
                now = soon
                continue
            _, g, name = min(spare)
        order.append((name, g))
        if name in FILL:
            filled.add((name, g))
            now += FILL[name][1]
            continue
        _, cost, link, way = CHAIN[at[g]]
        now += cost
        at[g] += 1
        ready[g] = now
        if link:
            links[link] = max(now, links[link]) + BUSY[link]
            ready[g] = links[link] + way
        if all(a > step_of["middle"] for a in at) and sums_ready is None:
            sums_ready = now
    order += [(name, 0) for name, _ in GAIN[summed:]]
    return order, now


def cols(head):
    return pl.ds(pl.multiple_of(head * D, D), D)


def mm(a, b, da, db):
    return lax.dot_general(a, b, (((da,), (db,)), ((), ())), preferred_element_type=F32)


def kernel(*refs):
    sources, (out, gq, gk, gv, gain_sum), refs = refs[:6], refs[6:11], refs[11:]
    (q, k, v, g_out, log_decay, gain, in_sems), refs = refs[:7], refs[7:]
    nd, ns, ng = len(Decays.scratch), len(Scan.scratch), len(Gain.scratch)
    total, cum, cums, inside, wts, weights, ga, gkp, gvp, gain_part, local, prior, later_local, later = refs[:14]
    refs = refs[14:]
    me = here()
    decays = Decays(me, refs[:nd], total)
    refs = refs[nd:]
    fore = Scan(me, refs[:ns], decays, prior, False)
    back = Scan(me, refs[ns : 2 * ns], decays, later, True)
    sums = Gain(me, refs[2 * ns :], gain_part, gain_sum)

    met = greet(me)
    held = (q, k, v, g_out, log_decay, gain)
    loads = [pltpu.make_async_copy(a, b, in_sems.at[n]) for n, (a, b) in enumerate(zip(sources, held))]
    for n in (4, 1, 2, 0, 3, 5):
        loads[n].start()
    loads[4].wait()
    upper = (
        lax.broadcasted_iota(jnp.int32, (T, T), 0) <= lax.broadcasted_iota(jnp.int32, (T, T), 1)
    ).astype(F32)
    running = lax.dot_general(
        log_decay[...], upper, (((1,), (0,)), ((), ())), precision=lax.Precision.HIGHEST, preferred_element_type=F32
    )
    cum[...] = running
    gain_part[...] = jnp.zeros_like(gain_part)
    blocks = jnp.broadcast_to(running[:, T - 1 : T], (HEADS, D))
    for j in range(NY):
        total[j] = blocks[j * OWN : (j + 1) * OWN]

    def for_heads(g, work, begin=0, end=NY, at_once=AT_ONCE):
        at_once = min(at_once, end - begin)

        def step(n, carry):
            for u in range(at_once):
                j = lax.rem(me["y"] + 1 + begin + n * at_once + u, NY)
                for i in range(HPG):
                    work(j, i, j * OWN + g * HPG + i)
            return carry

        if end - begin == at_once:
            step(0, 0)
        else:
            lax.fori_loop(0, (end - begin) // at_once, step, 0)

    def weight(head):
        by_row = cums[head]
        gap = jnp.concatenate([by_row, by_row[:, : T - D]], axis=1) - cum[pl.ds(head, 1), :]
        causal = lax.broadcasted_iota(jnp.int32, (T, T), 0) >= lax.broadcasted_iota(jnp.int32, (T, T), 1)
        return jnp.exp(jnp.where(causal, gap, -1e30))

    def end_scale(head):
        by_row = cums[head]
        return jnp.exp(by_row[T - 1 : T, :] - by_row)

    def local_of(g):
        def work(j, i, head):
            by_row = jnp.transpose(jnp.broadcast_to(cum[pl.ds(head, 1), :], (D, T)))
            cums[head] = by_row
            scale = jnp.exp(by_row[T - 1 : T, :] - by_row)
            decayed = (k[:, cols(head)].astype(F32) * scale).astype(BF)
            local[j, g, pl.ds(i * D, D), :] = mm(decayed, v[:, cols(head)], 0, 0).astype(BF)

        for_heads(g, work)

    def early(part, g):
        def work(j, i, head):
            scores = mm(q[:, cols(head)], k[:, cols(head)], 1, 1)
            factor = weight(head)
            weights[head] = factor
            weighted = (scores * factor).astype(BF)
            wts[head] = weighted
            inside[head] = mm(weighted, v[:, cols(head)], 1, 0)

        for_heads(g, work, NY // EARLY * part, NY // EARLY * (part + 1))

    def middle(g):
        fore.arrive(g)

        def work(j, i, head):
            state = prior[g, slot_of(me, "y", j), pl.ds(i * D, D), :]
            start = jnp.exp(cums[head])
            qh = q[:, cols(head)]
            attended = inside[head] + mm(qh, state, 1, 0) * start
            inv = lax.rsqrt(jnp.mean(attended * attended, axis=1, keepdims=True) + epsilon)
            normed = attended * inv
            row = gain[pl.ds(head, 1), :]
            out[:, cols(head)] = (normed * row).astype(BF)
            grad = g_out[:, cols(head)].astype(F32)
            scaled = grad * row
            lean = jnp.mean(scaled * normed, axis=1, keepdims=True)
            attended_grad = (inv * (scaled - normed * lean)).astype(BF)
            ga[head] = attended_grad
            gain_part[head // 4, pl.ds(lax.rem(head, 4), 1), :] = jnp.sum(grad * normed, axis=0, keepdims=True)
            decayed = (qh.astype(F32) * start).astype(BF)
            later_local[j, g, pl.ds(i * D, D), :] = mm(decayed, attended_grad, 0, 0).astype(BF)

        for_heads(g, work)
        back.start(g, later_local)

    def late(part, g):
        def work(j, i, head):
            grad = ga[head]
            grad_scores = mm(grad, v[:, cols(head)], 1, 1)
            gw = (grad_scores * weights[head]).astype(BF)
            state = prior[g, slot_of(me, "y", j), pl.ds(i * D, D), :]
            gq[:, cols(head)] = (mm(gw, k[:, cols(head)], 1, 0) + jnp.exp(cums[head]) * mm(grad, state, 1, 1)).astype(BF)
            gkp[head] = mm(gw, q[:, cols(head)], 0, 0)
            gvp[head] = mm(wts[head], grad, 0, 0)

        for_heads(g, work, NY // LATE * part, NY // LATE * (part + 1))

    def last(g):
        back.arrive(g)

        def work(j, i, head):
            state = later[g, slot_of(me, "y", j), pl.ds(i * D, D), :]
            scale = end_scale(head)
            gk[:, cols(head)] = (gkp[head] + scale * mm(v[:, cols(head)], state, 1, 1)).astype(BF)
            gv[:, cols(head)] = (gvp[head] + scale * mm(k[:, cols(head)], state, 1, 0)).astype(BF)

        for_heads(g, work)

    stages = {
        "lines": fore.over_lines,
        "planes": fore.over_planes,
        "before_lines": fore.before_lines,
        "before_blocks": fore.before_blocks,
        "middle": middle,
        "back_lines": back.over_lines,
        "back_planes": back.over_planes,
        "back_before_lines": back.before_lines,
        "back_before_blocks": back.before_blocks,
        "last": last,
    }
    for n in range(EARLY):
        stages[f"early{n}"] = functools.partial(early, n)
    for n in range(LATE):
        stages[f"late{n}"] = functools.partial(late, n)
    stages["gain"] = lambda g: sums.start()
    for axis in sums.AXES:
        stages[f"gain_{axis}"] = lambda g, axis=axis: sums.fold(axis)
    order, _ = plan()
    levels = [lambda: decays.lift("y", "x"), lambda: decays.lift("x", "z"), lambda: decays.settle("z")]
    needs = {"lines": 1, "planes": 2, "before_lines": 3}
    to_open = True
    loads[1].wait()
    loads[2].wait()
    for name, g in order:
        if name == "local":
            local_of(g)
            if to_open:
                met()
                decays.start()
                to_open = False
            fore.start(g, local)
            continue
        if name.startswith("early") and loads[0]:
            loads[0].wait()
            loads[0] = None
        if name == "middle" and loads[3]:
            loads[3].wait()
            loads[5].wait()
            loads[3] = None
        while levels and needs.get(name, 0) > 3 - len(levels):
            levels.pop(0)()
        stages[name](g)
        if name == "gain":
            fore.drain()
            decays.drain()
    back.drain()
    sums.drain()


PARTS = 4


def store_kernel(*refs):
    given, kept, sems = refs[:5], refs[5:10], refs[10]
    copies = [pltpu.make_async_copy(given[4], kept[4], sems.at[4 * PARTS])]
    for n in range(4):
        for p in range(PARTS):
            rows = pl.ds(p * (T // PARTS), T // PARTS)
            copies.append(pltpu.make_async_copy(given[n].at[rows], kept[n].at[rows], sems.at[n * PARTS + p]))
    for copy in copies:
        copy.start()
    for copy in copies:
        copy.wait()


def body(queries, key_vectors, value_vectors, out_grad, log_decay, norm_gain):
    shape = queries.shape
    wide = shape[-1]
    vmem = pl.BlockSpec(memory_space=pltpu.VMEM)
    scratch = [
        pltpu.VMEM((NY, OWN, D), F32),
        pltpu.VMEM((HEADS, T), F32),
        pltpu.VMEM((HEADS, T, D), F32),
        pltpu.VMEM((HEADS, T, D), F32),
        pltpu.VMEM((HEADS, T, T), BF),
        pltpu.VMEM((HEADS, T, T), F32),
        pltpu.VMEM((HEADS, T, D), BF),
        pltpu.VMEM((HEADS, T, D), F32),
        pltpu.VMEM((HEADS, T, D), F32),
        pltpu.VMEM((NZ, 8, D), F32),
        pltpu.VMEM((NY, G, R, D), BF),
        pltpu.VMEM((G, NY, R, D), BF),
        pltpu.VMEM((NY, G, R, D), BF),
        pltpu.VMEM((G, NY, R, D), BF),
    ]
    rows = (T, wide)
    last_row = (1, D // NY)
    hbm = pl.BlockSpec(memory_space=pltpu.HBM)
    results = pl.pallas_call(
        kernel,
        out_shape=[pltpu.VMEM(rows, BF)] * 4 + [pltpu.VMEM(last_row, F32)],
        in_specs=[hbm] * 6,
        out_specs=[vmem] * 5,
        scratch_shapes=[
            *[pltpu.VMEM(rows, BF)] * 4,
            pltpu.VMEM((HEADS, T), F32),
            pltpu.VMEM((HEADS, D), F32),
            pltpu.SemaphoreType.DMA((6,)),
            *scratch,
            *Decays.scratch,
            *Scan.scratch,
            *Scan.scratch,
            *Gain.scratch,
        ],
        compiler_params=pltpu.CompilerParams(
            collective_id=0, has_side_effects=True, vmem_limit_bytes=48 * 1024 * 1024
        ),
        name="attention",
    )(
        *[a.reshape(rows) for a in (queries, key_vectors, value_vectors, out_grad)],
        log_decay.reshape(HEADS, T),
        norm_gain.reshape(HEADS, D),
    )
    results = pl.pallas_call(
        store_kernel,
        out_shape=[jax.ShapeDtypeStruct(rows, BF)] * 4 + [jax.ShapeDtypeStruct(last_row, F32)],
        in_specs=[vmem] * 5,
        out_specs=[hbm] * 5,
        scratch_shapes=[pltpu.SemaphoreType.DMA((4 * PARTS + 1,))],
        compiler_params=pltpu.CompilerParams(vmem_limit_bytes=1024 * 1024),
        name="store",
    )(*results)
    return (*[r.reshape(shape) for r in results[:4]], results[4].reshape(D // NY))


def solution(mesh):
    split = Mesh(mesh.devices.reshape(NZ, NX, NY, mesh.shape["dp"]), AXES)
    rows = P("dp", SEQ, None)
    return jax.shard_map(
        body,
        mesh=split,
        in_specs=(rows, rows, rows, rows, P("dp", None, SEQ), P()),
        out_specs=(rows, rows, rows, rows, P(SEQ)),
        check_vma=False,
    )
```

time: 104 us -> 80.1 us (0.77)
  Pallas kernels: 94 us -> 79.2 us
  local copies, waits for them, and re-layouts: 8.43 us -> 0 us
    pallas_call x1 -> x2, Pallas kernels: 94 us -> 79.2 us  [the longest x1 76.5 us: body(): pl.pallas_call(kernel, out_shape=[pltpu.VMEM(rows, BF)] * 4 + [pltpu.VMEM...]
    unnamed x13 -> x0, local copies, waits for them, and re-layouts: 8.43 us -> none
where the time goes in v1:
time: 80.1 us; the launch traced here: 80 us
  Pallas kernels  79.2 us (99%)
    pallas_call x1, Pallas kernels, body(): pl.pallas_call(kernel, out_shape=[pltpu.VMEM(rows, BF)] * 4 + [pltpu.VMEM...  76.5 us
    pallas_call x1, Pallas kernels, body(): pl.pallas_call(store_kernel, out_shape=[jax.ShapeDtypeStruct(rows, BF)] *...  2.79 us

profile of v1, /device:TPU:2, one launch (start us, length us, event | category | flops | bytes accessed | tf_op | source)
XLA Modules:
  0.0 80.0 jit_solution(17246558514026764636)
XLA Ops:
  0.6 76.5 %attention.1 = (bf16[192,4096]{1,0:T(8,128)(2,1)S(1)}, bf16[192,4096]{1,0:T(8,128)(2,1)S(1)}, bf16[192,4096]{1,0:T(8,128)(2,1)S(1)}, bf16[192,4096]{1,0:T(8,128)(2,1)S(1)}, f32[1,32]{1,0:T(1,128)S(1)}) custom-call(bf16[192,4096]{1,0:T(8,128)(2,1)} %bitcast.11, bf16[192,4096]{1,0:T(8,128)(2,1)} %bitcast.12, bf16[192,4096]{1,0:T(8,128)(2,1)} %bitcast.13, ...), custom_call_target="tpu_custom_call" | custom-call | tf_op jit(solution)/shard_map/attention/pallas_call | solution.py:589
  77.1 2.8 %store.1 = (bf16[192,4096]{1,0:T(8,128)(2,1)}, bf16[192,4096]{1,0:T(8,128)(2,1)}, bf16[192,4096]{1,0:T(8,128)(2,1)}, bf16[192,4096]{1,0:T(8,128)(2,1)}, f32[1,32]{1,0:T(1,128)}) custom-call(bf16[192,4096]{1,0:T(8,128)(2,1)S(1)} %get-tuple-element.15.refs_0_, bf16[192,4096]{1,0:T(8,128)(2,1)S(1)} %get-tuple-element.16.refs_1_, ...), custom_call_target="tpu_custom_call" | custom-call | tf_op jit(solution)/shard_map/store/pallas_call | solution.py:614

commit v2 on v1

v2 whole, which is shorter than its diff:
```python
import functools

import jax
import jax.numpy as jnp
from jax import lax
from jax.experimental import pallas as pl
from jax.experimental.pallas import tpu as pltpu
from jax.sharding import Mesh
from jax.sharding import PartitionSpec as P

AXES = ("z", "x", "y", "dp")
SEQ = ("z", "x", "y")
SIZES = {"z": 8, "x": 4, "y": 4, "dp": 2}
NZ, NX, NY = 8, 4, 4
NP = NX * NY
D = 128
T = 192
HEADS = 2 * NP
NR = 2
RR = D // NR
UNITS = 2 * NR
BATCHES = 4
PER = NP // BATCHES
BF = jnp.bfloat16
F32 = jnp.float32
epsilon = 1e-06


def here():
    return {name: lax.axis_index(name) for name in AXES}


def plane_index(me):
    return me["x"] * NY + me["y"]


def shifted(me, **steps):
    return tuple(lax.rem(me[a] + steps[a], SIZES[a]) if a in steps else me[a] for a in AXES)


def push(src, dst, send, recv, target):
    return pltpu.make_async_remote_copy(
        src_ref=src,
        dst_ref=dst,
        send_sem=send,
        recv_sem=recv,
        device_id=target,
        device_id_type=pl.DeviceIdType.MESH,
    )


class Wire:
    def __init__(self, me, axis, sems):
        self.me, self.axis, self.sems = me, axis, sems
        self.peers = (NP if axis == "plane" else SIZES[axis]) - 1
        self.sent = {}

    def target(self, step):
        if self.axis == "plane":
            return shifted(self.me, x=step // NY, y=step % NY)
        return shifted(self.me, **{self.axis: step})

    def peer(self, step):
        to = self.target(step)
        if self.axis == "plane":
            return to[1] * NY + to[2]
        return to[AXES.index(self.axis)]

    def send(self, key, source, slots, steps=None):
        for step in steps or range(1, self.peers + 1):
            push(
                source(self.peer(step)),
                slots.at[step - 1],
                self.sems[0].at[key],
                self.sems[1].at[key],
                self.target(step),
            ).start()
        self.sent[key] = slots

    def _all(self, key, slots):
        taken = slots.at[pl.ds(0, self.peers)]
        return push(taken, taken, self.sems[0].at[key], self.sems[1].at[key], self.target(1))

    def arrived(self, key, slots):
        self._all(key, slots).wait_recv()

    def drain(self):
        for key, slots in self.sent.items():
            self._all(key, slots).wait_send()
        self.sent = {}


def sem_pair(keys):
    return [pltpu.SemaphoreType.DMA((keys,))] * 2


def slot_of(me, axis, index):
    if axis == "plane":
        dx = lax.rem(me["x"] + (NX - index // NY), NX)
        dy = lax.rem(me["y"] + (NY - index % NY), NY)
        return lax.rem(dx * NY + dy + (NP - 1), NP)
    n = SIZES[axis]
    return lax.rem(me[axis] + (n - 1) + (n - index), n)


def greet(me):
    barrier = pltpu.get_barrier_semaphore()
    targets = [shifted(me, z=step) for step in range(1, NZ)]
    targets += [shifted(me, x=step // NY, y=step % NY) for step in range(1, NP)]
    targets.append(shifted(me, dp=1))
    for target in targets:
        pl.semaphore_signal(barrier, inc=1, device_id=target, device_id_type=pl.DeviceIdType.MESH)
    return lambda: pl.semaphore_wait(barrier, len(targets))


class Decays:
    scratch = [*[pltpu.VMEM((n, 8, D), F32) for n in (NP, NZ, NP, NZ)], *sem_pair(1) * 2]

    def __init__(self, me, refs, total):
        self.me, self.total = me, total
        self.logs = {"plane": refs[0], "z": refs[1]}
        self.factors = {"plane": refs[2], "z": refs[3]}
        self.wires = {a: Wire(me, a, refs[4 + 2 * i : 6 + 2 * i]) for i, a in enumerate(("plane", "z"))}

    def start(self):
        logs = self.logs["plane"]
        self.wires["plane"].send(0, lambda peer: self.total.at[peer], logs)
        logs[NP - 1] = self.total[plane_index(self.me)]

    def lift(self):
        logs, above = self.logs["plane"], self.logs["z"]
        self.wires["plane"].arrived(0, logs)
        above[NZ - 1] = functools.reduce(jnp.add, [logs[k] for k in range(NP)])
        self.wires["z"].send(0, lambda peer: above.at[NZ - 1], above)
        self.factors["plane"][...] = jnp.exp(logs[...])

    def settle(self):
        self.wires["z"].arrived(0, self.logs["z"])
        self.factors["z"][...] = jnp.exp(self.logs["z"][...])

    def row(self, axis, slot, turn):
        return self.factors[axis][slot, turn : turn + 1, :]

    def drain(self):
        for wire in self.wires.values():
            wire.drain()


class Scan:
    scratch = [
        pltpu.VMEM((UNITS, NP, RR, D), BF),
        pltpu.VMEM((UNITS, NZ, RR, D), BF),
        pltpu.VMEM((UNITS, NP, RR, D), BF),
        *sem_pair(UNITS) * 3,
    ]

    def __init__(self, me, refs, decays, states, prior, backward):
        self.me, self.decays, self.states, self.prior, self.backward = me, decays, states, prior, backward
        self.given, self.planes, self.before = refs[:3]
        self.plane, self.z, self.back = [
            Wire(me, a, refs[3 + 2 * i : 5 + 2 * i]) for i, a in enumerate(("plane", "z", "plane"))
        ]

    def order(self, n):
        return list(range(n))[:: -1 if self.backward else 1]

    def mine(self, u, owner):
        return self.states.at[owner, u // NR, pl.ds(u % NR * RR, RR)]

    def start(self, u, steps):
        sent = [step for step in steps if step < NP]
        self.plane.send(u, lambda owner: self.mine(u, owner), self.given.at[u], sent)
        if len(sent) < len(steps):
            self.given[u, NP - 1] = self.states[plane_index(self.me), u // NR, pl.ds(u % NR * RR, RR), :]

    def over_plane(self, u):
        self.plane.arrived(u, self.given.at[u])
        total = None
        for k in self.order(NP):
            slot = slot_of(self.me, "plane", k)
            term = self.given[u, slot].astype(F32)
            total = term if total is None else total * self.decays.row("plane", slot, u // NR) + term
        self.planes[u, NZ - 1] = total.astype(BF)
        self.z.send(u, lambda peer: self.planes.at[u, NZ - 1], self.planes.at[u])

    def before_blocks(self, u):
        me = self.me
        self.z.arrived(u, self.planes.at[u])
        state = jnp.zeros((RR, D), F32)
        for k in self.order(NZ):
            slot = slot_of(me, "z", k)
            passed = (k > me["z"]) if self.backward else (k < me["z"])
            ahead = state * self.decays.row("z", slot, u // NR) + self.planes[u, slot].astype(F32)
            state = jnp.where(passed, ahead, state)
        for n, k in enumerate(self.order(NP)):
            self.before[u, k] = state.astype(BF)
            if n < NP - 1:
                slot = slot_of(me, "plane", k)
                state = state * self.decays.row("plane", slot, u // NR) + self.given[u, slot].astype(F32)
        self.back.send(u, lambda peer: self.before.at[u, peer], self.prior.at[u])
        self.prior[u, NP - 1] = self.before[u, plane_index(me)]

    def arrive(self, turn):
        for u in range(turn * NR, (turn + 1) * NR):
            self.back.arrived(u, self.prior.at[u])

    def state(self, turn, owner):
        slot = slot_of(self.me, "plane", owner)
        parts = [self.prior[turn * NR + r, slot] for r in range(NR)]
        return jnp.concatenate(parts, axis=0)

    def drain(self):
        for wire in (self.plane, self.z, self.back):
            wire.drain()


class Gain:
    AXES = ("z", "x", "y", "dp")
    scratch = [*[pltpu.VMEM((SIZES[a], 8, D), F32) for a in AXES], *sem_pair(1) * 4]

    def __init__(self, me, refs, part, out):
        self.me, self.part, self.out = me, part, out
        self.levels = dict(zip(self.AXES, refs[:4]))
        self.wires = {a: Wire(me, a, refs[4 + 2 * i : 6 + 2 * i]) for i, a in enumerate(self.AXES)}

    def start(self):
        self.wires["z"].send(0, lambda peer: self.part.at[peer], self.levels["z"])
        self.levels["z"][NZ - 1] = self.part[self.me["z"]]

    def fold(self, axis):
        n, level = SIZES[axis], self.levels[axis]
        self.wires[axis].arrived(0, level)
        total = functools.reduce(jnp.add, [level[slot_of(self.me, axis, k)] for k in range(n)])
        if axis != "dp":
            above = self.AXES[self.AXES.index(axis) + 1]
            held, m = self.levels[above], SIZES[above]
            held[m - 1] = total
            self.wires[above].send(0, lambda peer: held.at[m - 1], held)
            return
        width = D // NY
        mine = lax.broadcasted_iota(jnp.int32, (8, D), 0) == self.me["x"]
        row = jnp.sum(jnp.where(mine, total, 0.0), axis=0, keepdims=True)
        self.out[...] = functools.reduce(
            jnp.add,
            [jnp.where(self.me["y"] == k, row[:, k * width : (k + 1) * width], 0.0) for k in range(NY)],
        )

    def drain(self):
        for wire in self.wires.values():
            wire.drain()


COST = {"plane": 0.15, "blocks": 0.25, "middle": 1.05, "last": 0.3, "early": 0.52, "late": 1.3}
COST |= {"bplane": 0.15, "bblocks": 0.25}
BUSY = 11.3 / UNITS
WAY = {"exch": 4.5, "z": 4.3, "ret": 3.5}
GAIN = (("gain", 4.8), ("gain_z", 4.0), ("gain_x", 4.0), ("gain_y", 2.0), ("gain_dp", 0.0))
MARGIN = 2.0


def plan():
    units = lambda turn: range(turn * NR, (turn + 1) * NR)
    batches = [(turn, b) for turn in range(2) for b in range(BATCHES)]
    needs, rank = {}, {}
    for u in range(UNITS):
        needs["plane", u] = [("exch", u)]
        needs["blocks", u] = [("z", u)]
        needs["bplane", u] = [("bexch", u)]
        needs["bblocks", u] = [("bz", u)]
    for turn, b in batches:
        key = turn * BATCHES + b
        needs["early", key] = []
        needs["middle", key] = [("ret", u) for u in units(turn)] + [("early", key)]
        needs["late", key] = [("middle", key)]
        needs["last", key] = [("bret", u) for u in units(turn)] + [("late", key)]
    before = None
    for name, _ in GAIN:
        needs[name, 0] = [before] if before else [("middle", n) for n in range(2 * BATCHES)]
        before = (name, 0)
    order_of = ["plane", "blocks", "bplane", "bblocks", "middle", "last"]
    links = {"plane": 0.0, "z": 0.0}
    done = {}
    now = 0.0

    def send(what, link, share, way):
        links[link] = max(now, links[link]) + BUSY * share
        done[what] = links[link] + way

    for u in range(UNITS):
        send(("exch", u), "plane", 1, WAY["exch"])
    order, left = [], dict(needs)
    while left:
        at = {k: max([done.get(d, 1e9) for d in v], default=0.0) for k, v in left.items()}
        fits = [
            (order_of.index(k[0]), k[1], k) for k in left if k[0] in order_of and at[k] <= now
        ]
        sums = [k for k in left if k[0].startswith("gain") and at[k] <= now]
        known = [at[k] for k in left if now < at[k] < 1e8]
        soon = min([at[k] for k in left if k[0] in order_of and now < at[k] < 1e8], default=1e9)
        if not fits:
            for k in left:
                if k[0] in ("middle", "last"):
                    filler = ("early" if k[0] == "middle" else "late", k[1])
                    rest = [d for d in needs[k] if d != filler]
                    if filler in left and at[filler] <= now and all(done.get(d, 1e9) <= now for d in rest):
                        fits.append((9, k[1], filler))
        if fits:
            pick = min(fits)[2]
        elif sums:
            pick = sums[0]
        else:
            spare = [
                (k[0] == "late", k[1], k)
                for k in left
                if k[0] in ("early", "late") and at[k] <= now and (now + COST[k[0]] <= soon + 0.15 or soon >= 1e8)
            ]
            if not spare:
                now = min(known)
                continue
            pick = min(spare)[2]
        name, key = pick
        order.append(pick)
        del left[pick]
        now += COST.get(name, 0.1)
        done[pick] = now
        if name.startswith("gain"):
            done[pick] = now + dict(GAIN)[name] + MARGIN
        if name in ("plane", "bplane"):
            send(("z" if name == "plane" else "bz", key), "z", 1, WAY["z"])
        if name in ("blocks", "bblocks"):
            send(("ret" if name == "blocks" else "bret", key), "plane", 1, WAY["ret"])
        if name == "middle":
            turn, b = divmod(key, BATCHES)
            first, *others = units(turn)
            send(("bexch", first), "plane", 1 / BATCHES, WAY["exch"])
            if b < BATCHES - 1:
                done.pop(("bexch", first))
            else:
                for u in others:
                    send(("bexch", u), "plane", 1, WAY["exch"])
    return order, now


def cols(head):
    return pl.ds(pl.multiple_of(head * D, D), D)


def mm(a, b, da, db):
    return lax.dot_general(a, b, (((da,), (db,)), ((), ())), preferred_element_type=F32)


def kernel(*refs):
    sources, (out, gq, gk, gv, gain_sum), refs = refs[:6], refs[6:11], refs[11:]
    (q, k, v, g_out, log_decay, gain, in_sems), refs = refs[:7], refs[7:]
    nd, ns = len(Decays.scratch), len(Scan.scratch)
    total, cum, cums, inside, wts, weights, ga, gkp, gvp, gain_part, local, prior, later_local, later = refs[:14]
    refs = refs[14:]
    me = here()
    decays = Decays(me, refs[:nd], total)
    refs = refs[nd:]
    fore = Scan(me, refs[:ns], decays, local, prior, False)
    back = Scan(me, refs[ns : 2 * ns], decays, later_local, later, True)
    sums = Gain(me, refs[2 * ns :], gain_part, gain_sum)

    met = greet(me)
    held = (q, k, v, g_out, log_decay, gain)
    loads = [pltpu.make_async_copy(a, b, in_sems.at[n]) for n, (a, b) in enumerate(zip(sources, held))]
    for n in (4, 1, 2, 0, 3, 5):
        loads[n].start()
    loads[4].wait()
    upper = (
        lax.broadcasted_iota(jnp.int32, (T, T), 0) <= lax.broadcasted_iota(jnp.int32, (T, T), 1)
    ).astype(F32)
    running = lax.dot_general(
        log_decay[...], upper, (((1,), (0,)), ((), ())), precision=lax.Precision.HIGHEST, preferred_element_type=F32
    )
    cum[...] = running
    gain_part[...] = jnp.zeros_like(gain_part)
    total[...] = jnp.zeros_like(total)
    blocks = jnp.broadcast_to(running[:, T - 1 : T], (HEADS, D))
    for o in range(NP):
        total[o, 0:2, :] = blocks[2 * o : 2 * o + 2]

    def for_heads(turn, work, begin=0, end=NP, at_once=4):
        at_once = min(at_once, end - begin)

        def step(n, carry):
            for u in range(at_once):
                s = begin + n * at_once + u + 1
                x = lax.rem(me["x"] + s // NY, NX)
                y = lax.rem(me["y"] + s % NY, NY)
                owner = x * NY + y
                work(owner, 2 * owner + turn)
            return carry

        if end - begin == at_once:
            step(0, 0)
        else:
            lax.fori_loop(0, (end - begin) // at_once, step, 0)

    def batch(key):
        turn, b = divmod(key, BATCHES)
        return turn, b * PER, (b + 1) * PER

    def weight(head):
        by_row = cums[head]
        gap = jnp.concatenate([by_row, by_row[:, : T - D]], axis=1) - cum[pl.ds(head, 1), :]
        causal = lax.broadcasted_iota(jnp.int32, (T, T), 0) >= lax.broadcasted_iota(jnp.int32, (T, T), 1)
        return jnp.exp(jnp.where(causal, gap, -1e30))

    def end_scale(head):
        by_row = cums[head]
        return jnp.exp(by_row[T - 1 : T, :] - by_row)

    def local_of(turn):
        def work(owner, head):
            by_row = jnp.transpose(jnp.broadcast_to(cum[pl.ds(head, 1), :], (D, T)))
            cums[head] = by_row
            scale = jnp.exp(by_row[T - 1 : T, :] - by_row)
            decayed = (k[:, cols(head)].astype(F32) * scale).astype(BF)
            local[owner, turn] = mm(decayed, v[:, cols(head)], 0, 0).astype(BF)

        for_heads(turn, work)

    def early(key):
        turn, begin, end = batch(key)

        def work(owner, head):
            scores = mm(q[:, cols(head)], k[:, cols(head)], 1, 1)
            factor = weight(head)
            weights[head] = factor
            weighted = (scores * factor).astype(BF)
            wts[head] = weighted
            inside[head] = mm(weighted, v[:, cols(head)], 1, 0)

        for_heads(turn, work, begin, end)

    def middle(key):
        turn, begin, end = batch(key)
        if begin == 0:
            fore.arrive(turn)

        def work(owner, head):
            state = fore.state(turn, owner)
            start = jnp.exp(cums[head])
            qh = q[:, cols(head)]
            attended = inside[head] + mm(qh, state, 1, 0) * start
            inv = lax.rsqrt(jnp.mean(attended * attended, axis=1, keepdims=True) + epsilon)
            normed = attended * inv
            row = gain[pl.ds(head, 1), :]
            out[:, cols(head)] = (normed * row).astype(BF)
            grad = g_out[:, cols(head)].astype(F32)
            scaled = grad * row
            lean = jnp.mean(scaled * normed, axis=1, keepdims=True)
            attended_grad = (inv * (scaled - normed * lean)).astype(BF)
            ga[head] = attended_grad
            gain_part[head // 4, pl.ds(lax.rem(head, 4), 1), :] = jnp.sum(grad * normed, axis=0, keepdims=True)
            decayed = (qh.astype(F32) * start).astype(BF)
            later_local[owner, turn] = mm(decayed, attended_grad, 0, 0).astype(BF)

        for_heads(turn, work, begin, end)
        back.start(turn * NR, range(begin + 1, end + 1))
        if end == NP:
            for r in range(1, NR):
                back.start(turn * NR + r, range(1, NP + 1))

    def late(key):
        turn, begin, end = batch(key)

        def work(owner, head):
            grad = ga[head]
            grad_scores = mm(grad, v[:, cols(head)], 1, 1)
            gw = (grad_scores * weights[head]).astype(BF)
            state = fore.state(turn, owner)
            gq[:, cols(head)] = (mm(gw, k[:, cols(head)], 1, 0) + jnp.exp(cums[head]) * mm(grad, state, 1, 1)).astype(BF)
            gkp[head] = mm(gw, q[:, cols(head)], 0, 0)
            gvp[head] = mm(wts[head], grad, 0, 0)

        for_heads(turn, work, begin, end)

    def last(key):
        turn, begin, end = batch(key)
        if begin == 0:
            back.arrive(turn)

        def work(owner, head):
            state = back.state(turn, owner)
            scale = end_scale(head)
            gk[:, cols(head)] = (gkp[head] + scale * mm(v[:, cols(head)], state, 1, 1)).astype(BF)
            gv[:, cols(head)] = (gvp[head] + scale * mm(k[:, cols(head)], state, 1, 0)).astype(BF)

        for_heads(turn, work, begin, end)

    stages = {
        "early": early,
        "plane": fore.over_plane,
        "blocks": fore.before_blocks,
        "middle": middle,
        "late": late,
        "bplane": back.over_plane,
        "bblocks": back.before_blocks,
        "last": last,
        "gain": lambda key: sums.start(),
    }
    for axis in sums.AXES:
        stages[f"gain_{axis}"] = lambda key, axis=axis: sums.fold(axis)
    loads[1].wait()
    loads[2].wait()
    local_of(0)
    met()
    decays.start()
    for u in range(NR):
        fore.start(u, range(1, NP + 1))
    local_of(1)
    for u in range(NR, UNITS):
        fore.start(u, range(1, NP + 1))
    first = {"early": lambda: loads[0].wait(), "plane": decays.lift, "blocks": decays.settle}
    first["middle"] = lambda: (loads[3].wait(), loads[5].wait())
    first["gain"] = lambda: (fore.drain(), decays.drain())
    for name, g in plan()[0]:
        first.pop(name, lambda: None)()
        stages[name](g)
    back.drain()
    sums.drain()


PARTS = 4


def store_kernel(*refs):
    given, kept, sems = refs[:5], refs[5:10], refs[10]
    copies = [pltpu.make_async_copy(given[4], kept[4], sems.at[4 * PARTS])]
    for n in range(4):
        for p in range(PARTS):
            rows = pl.ds(p * (T // PARTS), T // PARTS)
            copies.append(pltpu.make_async_copy(given[n].at[rows], kept[n].at[rows], sems.at[n * PARTS + p]))
    for copy in copies:
        copy.start()
    for copy in copies:
        copy.wait()


def body(queries, key_vectors, value_vectors, out_grad, log_decay, norm_gain):
    shape = queries.shape
    rows = (T, shape[-1])
    last_row = (1, D // NY)
    vmem = pl.BlockSpec(memory_space=pltpu.VMEM)
    hbm = pl.BlockSpec(memory_space=pltpu.HBM)
    scratch = [
        pltpu.VMEM((NP, 8, D), F32),
        pltpu.VMEM((HEADS, T), F32),
        pltpu.VMEM((HEADS, T, D), F32),
        pltpu.VMEM((HEADS, T, D), F32),
        pltpu.VMEM((HEADS, T, T), BF),
        pltpu.VMEM((HEADS, T, T), F32),
        pltpu.VMEM((HEADS, T, D), BF),
        pltpu.VMEM((HEADS, T, D), F32),
        pltpu.VMEM((HEADS, T, D), F32),
        pltpu.VMEM((NZ, 8, D), F32),
        pltpu.VMEM((NP, 2, D, D), BF),
        pltpu.VMEM((UNITS, NP, RR, D), BF),
        pltpu.VMEM((NP, 2, D, D), BF),
        pltpu.VMEM((UNITS, NP, RR, D), BF),
    ]
    results = pl.pallas_call(
        kernel,
        out_shape=[pltpu.VMEM(rows, BF)] * 4 + [pltpu.VMEM(last_row, F32)],
        in_specs=[hbm] * 6,
        out_specs=[vmem] * 5,
        scratch_shapes=[
            *[pltpu.VMEM(rows, BF)] * 4,
            pltpu.VMEM((HEADS, T), F32),
            pltpu.VMEM((HEADS, D), F32),
            pltpu.SemaphoreType.DMA((6,)),
            *scratch,
            *Decays.scratch,
            *Scan.scratch,
            *Scan.scratch,
            *Gain.scratch,
        ],
        compiler_params=pltpu.CompilerParams(
            collective_id=0, has_side_effects=True, vmem_limit_bytes=48 * 1024 * 1024
        ),
        name="attention",
    )(
        *[a.reshape(rows) for a in (queries, key_vectors, value_vectors, out_grad)],
        log_decay.reshape(HEADS, T),
        norm_gain.reshape(HEADS, D),
    )
    results = pl.pallas_call(
        store_kernel,
        out_shape=[jax.ShapeDtypeStruct(rows, BF)] * 4 + [jax.ShapeDtypeStruct(last_row, F32)],
        in_specs=[vmem] * 5,
        out_specs=[hbm] * 5,
        scratch_shapes=[pltpu.SemaphoreType.DMA((4 * PARTS + 1,))],
        compiler_params=pltpu.CompilerParams(vmem_limit_bytes=1024 * 1024),
        name="store",
    )(*results)
    return (*[r.reshape(shape) for r in results[:4]], results[4].reshape(D // NY))


def solution(mesh):
    split = Mesh(mesh.devices.reshape(NZ, NX, NY, mesh.shape["dp"]), AXES)
    rows = P("dp", SEQ, None)
    return jax.shard_map(
        body,
        mesh=split,
        in_specs=(rows, rows, rows, rows, P("dp", None, SEQ), P()),
        out_specs=(rows, rows, rows, rows, P(SEQ)),
        check_vma=False,
    )
```

time: 80.1 us -> 70.2 us (0.88); the launches traced: 80 us -> 69 us
  Pallas kernels: 79.2 us -> 68.2 us
    pallas_call x1, Pallas kernels: 76.5 us -> 65.4 us  [body(): pl.pallas_call(kernel, out_shape=[pltpu.VMEM(rows, BF)] * 4 + [pltpu.VMEM...]
where the time goes in v2:
time: 70.2 us; the launch traced here: 69 us
  Pallas kernels  68.2 us (97%)
  between operations  0.8 us (1%)
    pallas_call x1, Pallas kernels, body(): pl.pallas_call(kernel, out_shape=[pltpu.VMEM(rows, BF)] * 4 + [pltpu.VMEM...  65.4 us
    pallas_call x1, Pallas kernels, body(): pl.pallas_call(store_kernel, out_shape=[jax.ShapeDtypeStruct(rows, BF)] *...  2.79 us

profile of v2, /device:TPU:2, one launch (start us, length us, event | category | flops | bytes accessed | tf_op | source)
XLA Modules:
  0.0 69.0 jit_solution(8920348639440300887)
XLA Ops:
  0.6 65.4 %attention.1 = (bf16[192,4096]{1,0:T(8,128)(2,1)S(1)}, bf16[192,4096]{1,0:T(8,128)(2,1)S(1)}, bf16[192,4096]{1,0:T(8,128)(2,1)S(1)}, bf16[192,4096]{1,0:T(8,128)(2,1)S(1)}, f32[1,32]{1,0:T(1,128)S(1)}) custom-call(bf16[192,4096]{1,0:T(8,128)(2,1)} %bitcast.11, bf16[192,4096]{1,0:T(8,128)(2,1)} %bitcast.12, bf16[192,4096]{1,0:T(8,128)(2,1)} %bitcast.13, ...), custom_call_target="tpu_custom_call" | custom-call | tf_op jit(solution)/shard_map/attention/pallas_call | solution.py:565
  66.1 2.8 %store.1 = (bf16[192,4096]{1,0:T(8,128)(2,1)}, bf16[192,4096]{1,0:T(8,128)(2,1)}, bf16[192,4096]{1,0:T(8,128)(2,1)}, bf16[192,4096]{1,0:T(8,128)(2,1)}, f32[1,32]{1,0:T(1,128)}) custom-call(bf16[192,4096]{1,0:T(8,128)(2,1)S(1)} %get-tuple-element.15.refs_0_, bf16[192,4096]{1,0:T(8,128)(2,1)S(1)} %get-tuple-element.16.refs_1_, ...), custom_call_target="tpu_custom_call" | custom-call | tf_op jit(solution)/shard_map/store/pallas_call | solution.py:590
